TPU v7x, 32 devices: a whole 2x2x4 slice. The times are simulated.
32 devices in a mesh: head: 4 (over z), seq: 8 (over y, x, core).
Axes of the slice: x: 2, y: 2, z: 4, core: 2. Of those that a mesh axis runs over, the one named last changes fastest.
Arguments:
- queries: bfloat16 [1024, 8192], P('seq', 'head'), may hold values from -100 to 100
- keys: bfloat16 [1024, 1024], P('seq', 'head'), may hold values from -5 to 5
- values: bfloat16 [1024, 1024], P('seq', 'head'), may hold values from -6 to 6
- q_tangent: bfloat16 [1024, 8192], P('seq', 'head'), may hold values from -6 to 6
- k_tangent: bfloat16 [1024, 1024], P('seq', 'head'), may hold values from -6 to 6
- v_tangent: bfloat16 [1024, 1024], P('seq', 'head'), may hold values from -6 to 6
- out_grad: bfloat16 [1024, 8192], P('seq', 'head'), may hold values from -6 to 6
- block_order: int32 [8], replicated, may hold values from 0 to 7, each once
Outputs:
- dq_tangent: bfloat16 [1024, 8192], P('seq', 'head')
- dk_tangent: bfloat16 [1024, 1024], P('seq', 'head')
- dv_tangent: bfloat16 [1024, 1024], P('seq', 'head')
- squared_norm: float32 [], replicated
Inputs may be any that keep to these rules, and one draw needn't show every extreme that they name: `block_order`: every value of 0 to 7 appears once.
All inputs are finite; a program needn't handle non-finite values.
Results may differ from a plain program's by a relative error of at most 0.025.
Values may be sent and summed in bfloat16 or wider, within the bound.
No kernel may reach another device: no remote copies, remote signals or barrier semaphores. Data moves between devices by JAX's collectives and lax.ppermute only.
A program may use at most 64 MiB of HBM per device.

v0:
```python
import jax
import jax.numpy as jnp
from jax import lax
from jax.sharding import PartitionSpec as P

HD = 128
G = 8
neg_fill = -1e30


def body(queries, keys, values, q_tangent, k_tangent, v_tangent, out_grad, block_order):
    tokens = queries.shape[0]
    heads = keys.shape[1] // HD
    scaling = HD ** (-0.5)
    shards = lax.axis_size("seq")
    my_index = lax.axis_index("seq")
    my_block = block_order[my_index]
    query_pos = my_block * tokens + jnp.arange(tokens, dtype=jnp.int32)
    query_rows = queries.reshape(tokens, heads, G, HD)
    query_tan = q_tangent.reshape(tokens, heads, G, HD)
    grad_rows = out_grad.reshape(tokens, heads, G, HD)

    def block_scores(blocks, key_pos):
        key_blk, val_blk, key_tan, val_tan = [b.reshape(b.shape[0], heads, HD) for b in blocks]
        visible = (key_pos[None, :] <= query_pos[:, None])[None, None]
        s_main = (
            jnp.einsum("thgd,shd->hgts", query_rows, key_blk, preferred_element_type=jnp.float32)
            * scaling
        )
        s_tan = (
            jnp.einsum("thgd,shd->hgts", query_tan, key_blk, preferred_element_type=jnp.float32)
            + jnp.einsum("thgd,shd->hgts", query_rows, key_tan, preferred_element_type=jnp.float32)
        ) * scaling
        d_prob = jnp.einsum(
            "thgd,shd->hgts", grad_rows, val_blk, preferred_element_type=jnp.float32
        )
        d_prob_tan = jnp.einsum(
            "thgd,shd->hgts", grad_rows, val_tan, preferred_element_type=jnp.float32
        )
        return (visible, s_main, s_tan, d_prob, d_prob_tan, key_blk, key_tan)

    def add_stats(row_stats, blocks, key_pos):
        visible, s_main, s_tan, d_prob, d_prob_tan, key_blk, key_tan = block_scores(blocks, key_pos)
        row_max, row_total, tan_sum, grad_sum, cross_sum, extra_sum = row_stats
        new_max = jnp.maximum(row_max, jnp.max(jnp.where(visible, s_main, neg_fill), axis=-1))
        decay = jnp.exp(row_max - new_max)
        expo = jnp.where(visible, jnp.exp(s_main - new_max[..., None]), 0.0)
        return (
            new_max,
            row_total * decay + jnp.sum(expo, axis=-1),
            tan_sum * decay + jnp.sum(expo * s_tan, axis=-1),
            grad_sum * decay + jnp.sum(expo * d_prob, axis=-1),
            cross_sum * decay + jnp.sum(expo * s_tan * d_prob, axis=-1),
            extra_sum * decay + jnp.sum(expo * d_prob_tan, axis=-1),
        )

    def block_grads(finished, blocks, key_pos):
        visible, s_main, s_tan, d_prob, d_prob_tan, key_blk, key_tan = block_scores(blocks, key_pos)
        row_max, row_total, tan_mean, delta, delta_tan = [f[..., None] for f in finished]
        prob = jnp.where(visible, jnp.exp(s_main - row_max), 0.0) / row_total
        prob_tan = prob * (s_tan - tan_mean)
        d_score = prob * (d_prob - delta)
        d_score_tan = prob_tan * (d_prob - delta) + prob * (d_prob_tan - delta_tan)
        prob_tan_b = prob_tan.astype(jnp.bfloat16)
        d_score_b = d_score.astype(jnp.bfloat16)
        d_score_tan_b = d_score_tan.astype(jnp.bfloat16)
        dq_part = (
            jnp.einsum("hgts,shd->thgd", d_score_tan_b, key_blk, preferred_element_type=jnp.float32)
            + jnp.einsum("hgts,shd->thgd", d_score_b, key_tan, preferred_element_type=jnp.float32)
        ) * scaling
        dk_part = (
            jnp.einsum(
                "hgts,thgd->shd", d_score_tan_b, query_rows, preferred_element_type=jnp.float32
            )
            + jnp.einsum("hgts,thgd->shd", d_score_b, query_tan, preferred_element_type=jnp.float32)
        ) * scaling
        dv_part = jnp.einsum(
            "hgts,thgd->shd", prob_tan_b, grad_rows, preferred_element_type=jnp.float32
        )
        key_rows = key_pos.shape[0]
        return (
            dq_part,
            dk_part.reshape(key_rows, heads * HD),
            dv_part.reshape(key_rows, heads * HD),
        )

    row_zero = jnp.zeros((heads, G, tokens), jnp.float32)
    start_stats = (
        jnp.full((heads, G, tokens), neg_fill, jnp.float32),
        row_zero,
        row_zero,
        row_zero,
        row_zero,
        row_zero,
    )
    dq_zero = jnp.zeros((tokens, heads, G, HD), jnp.float32)
    whole = (
        lax.all_gather(keys, "seq", axis=0, tiled=True),
        lax.all_gather(values, "seq", axis=0, tiled=True),
        lax.all_gather(k_tangent, "seq", axis=0, tiled=True),
        lax.all_gather(v_tangent, "seq", axis=0, tiled=True),
    )
    inverse = (
        jnp.zeros((shards,), jnp.int32).at[block_order].set(jnp.arange(shards, dtype=jnp.int32))
    )
    all_rows = shards * tokens
    ordered = tuple((w.reshape(shards, tokens, -1)[inverse].reshape(all_rows, -1) for w in whole))
    block_rows = min(512, all_rows)
    visits = (my_block * tokens + tokens + block_rows - 1) // block_rows

    def slice_blocks(block_index):
        offset = block_index * block_rows
        pieces = tuple((lax.dynamic_slice_in_dim(o, offset, block_rows, 0) for o in ordered))
        return (pieces, offset + jnp.arange(block_rows, dtype=jnp.int32))

    def stats_turn(block_index, row_stats):
        pieces, key_pos = slice_blocks(block_index)
        return add_stats(row_stats, pieces, key_pos)

    row_max, row_total, tan_sum, grad_sum, cross_sum, extra_sum = lax.fori_loop(
        0, visits, stats_turn, start_stats
    )
    tan_mean = tan_sum / row_total
    delta = grad_sum / row_total
    delta_tan = cross_sum / row_total - tan_mean * delta + extra_sum / row_total
    finished = (row_max, row_total, tan_mean, delta, delta_tan)

    def grad_turn(block_index, carry):
        dq_acc, dk_sorted, dv_sorted = carry
        pieces, key_pos = slice_blocks(block_index)
        dq_part, dk_part, dv_part = block_grads(finished, pieces, key_pos)
        offset = block_index * block_rows
        return (
            dq_acc + dq_part,
            lax.dynamic_update_slice_in_dim(dk_sorted, dk_part, offset, 0),
            lax.dynamic_update_slice_in_dim(dv_sorted, dv_part, offset, 0),
        )

    side_zero = jnp.zeros((all_rows, heads * HD), jnp.float32)
    dq_acc, dk_sorted, dv_sorted = lax.fori_loop(
        0, visits, grad_turn, (dq_zero, side_zero, side_zero)
    )
    dk_local = dk_sorted.reshape(shards, tokens, -1)[block_order].reshape(all_rows, -1)
    dv_local = dv_sorted.reshape(shards, tokens, -1)[block_order].reshape(all_rows, -1)
    dk_total, dv_total = (
        lax.psum_scatter(
            dk_local.astype(jnp.bfloat16), "seq", scatter_dimension=0, tiled=True
        ).astype(jnp.float32),
        lax.psum_scatter(
            dv_local.astype(jnp.bfloat16), "seq", scatter_dimension=0, tiled=True
        ).astype(jnp.float32),
    )
    dq_out = dq_acc.reshape(tokens, heads * G * HD).astype(jnp.bfloat16)
    dk_out = dk_total.astype(jnp.bfloat16)
    dv_out = dv_total.astype(jnp.bfloat16)
    dq_wide = dq_out.astype(jnp.float32)
    dk_wide = dk_out.astype(jnp.float32)
    dv_wide = dv_out.astype(jnp.float32)
    local_term = (
        jnp.sum(dq_wide * dq_wide) + jnp.sum(dk_wide * dk_wide) + jnp.sum(dv_wide * dv_wide)
    )
    squared_norm = lax.psum(local_term, ("head", "seq"))
    return (dq_out, dk_out, dv_out, squared_norm)


def solution(mesh):
    placed = (
        P("seq", "head"),
        P("seq", "head"),
        P("seq", "head"),
        P("seq", "head"),
        P("seq", "head"),
        P("seq", "head"),
        P("seq", "head"),
        P(),
    )
    return jax.shard_map(
        body,
        mesh=mesh,
        in_specs=placed,
        out_specs=(P("seq", "head"), P("seq", "head"), P("seq", "head"), P()),
        check_vma=False,
    )
```

profile of v0, /device:TPU:0, one launch (start us, length us, event | category | flops | bytes accessed | tf_op | source)
XLA Modules:
  0.0 250.2 jit_solution(16309284983064121922)
XLA Ops:
  11.0 11.6 %all_gather.13 = bf16[1024,256]{1,0:T(8,128)(2,1)S(1)} all-gather(bf16[128,256]{1,0:T(8,128)(2,1)} %param.16), channel_id=1, replica_groups=mesh['head'=4,'seq'=8] {'seq'}, dimensions={0}, use_global_device_ids=true | all-gather | bytes 589824 | tf_op jit(solution)/shard_map/all_gather | solution.py:100
  23.5 9.7 %all_gather.14 = bf16[1024,256]{1,0:T(8,128)(2,1)S(1)} all-gather(bf16[128,256]{1,0:T(8,128)(2,1)} %param.14), channel_id=1, replica_groups=mesh['head'=4,'seq'=8] {'seq'}, dimensions={0}, use_global_device_ids=true | all-gather | bytes 589824 | tf_op jit(solution)/shard_map/all_gather | solution.py:99
  34.8 9.2 %all_gather.15 = bf16[1024,256]{1,0:T(8,128)(2,1)S(1)} all-gather(bf16[128,256]{1,0:T(8,128)(2,1)S(1)} %copy-done.16), channel_id=1, replica_groups=mesh['head'=4,'seq'=8] {'seq'}, dimensions={0}, use_global_device_ids=true | all-gather | bytes 589824 | tf_op jit(solution)/shard_map/all_gather | solution.py:101
  45.6 9.5 %all_gather.12 = bf16[1024,256]{1,0:T(8,128)(2,1)S(1)} all-gather(bf16[128,256]{1,0:T(8,128)(2,1)S(1)} %copy-done.17), channel_id=1, replica_groups=mesh['head'=4,'seq'=8] {'seq'}, dimensions={0}, use_global_device_ids=true | all-gather | bytes 589824 | tf_op jit(solution)/shard_map/all_gather | solution.py:98
  60.2 7.8 %while.36 = (s32[]{:T(128)}, f32[2,8,128]{2,1,0:T(8,128)S(1)}, f32[2,8,128]{2,1,0:T(8,128)S(1)}, f32[2,8,128]{2,1,0:T(8,128)S(1)}, f32[2,8,128]{2,1,0:T(8,128)S(...) while((s32[]{:T(128)}, f32[2,8,128]{2,1,0:T(8,128)S(1)}, ...), condition=%wide.region_8.9_spmd.clone, body=%wide.region_1.8_spmd.clone.sunk | while | flops 1366372992 | bytes 46478664 | solution.py:120
  63.0 1.5 bitcast_multiply_fusion.5
  64.6 2.1 fusion.114
  70.8 23.7 %while.37 = (s32[]{:T(128)}, f32[128,2,8,128]{0,3,2,1:T(8,128)}, bf16[1024,256]{1,0:T(8,128)(2,1)}, bf16[1024,256]{1,0:T(8,128)(2,1)}, s32[]{:T(128)}, /*index=5...) while((s32[]{:T(128)}, f32[128,2,8,128]{0,3,2,1:T(8,128)}, ...), condition=%wide.region_10.11_spmd.clone, body=%wide.region_9.10_spmd.clone.sunk | while | flops 2704474624 | bytes 123131472 | solution.py:140
  73.0 1.7 multiply_convert_fusion.2
  78.4 1.8 convolution_bitcast_fusion.3
  80.3 1.5 fusion.143
  81.8 1.8 copy.153
  83.6 3.7 %fusion.142 = bf16[2,512,128,1]{1,2,3,0:T(8,128)(2,1)} fusion(bf16[128,2,8,128]{0,3,2,1:T(8,128)(2,1)S(1)} %get-tuple-element.796, f32[2,8,128,512]{2,3,1,0:T(8,128)} %copy-done), kind=kOutput, calls=%fused_computation.47.clone.1 | convolution fusion | flops 269484032 | bytes 4980736 | tf_op jit(solution)/shard_map/while/body/hgts,thgd->shd/dot_general | solution.py:77
  87.3 1.8 copy.152
  89.1 2.0 constant_dynamic-update-slice_fusion.3
  91.6 2.9 %fusion.141 = f32[128,2,8,128]{0,3,2,1:T(8,128)} fusion(f32[128,2,8,128]{0,3,2,1:T(8,128)} %get-tuple-element.762, f32[2,128,8,128]{3,1,2,0:T(8,128)S(1)} %fusion.140, bf16[512,2,128,1]{0,2,3,1:T(8,128)(2,1)S(1)} %bitcast.291, bf16[2,8,128,512]{2,3,1,0:T(8,128)(2,1)S(1)} %copy-done.2), kind=kOutput, calls=%fused_computation.52.clone.1 | convolution fusion | flops 269221888 | bytes 5505024 | tf_op jit(solution)/shard_map/while/body/hgts,shd->thgd/dot_general | solution.py:69
  94.5 2.5 %gather_fusion.4 = bf16[8,128,256]{2,1,0:T(8,128)(2,1)} fusion(bf16[8,128,256]{2,1,0:T(8,128)(2,1)} %bitcast.302, s32[1024]{0:T(1024)} %pad_clamp_fusion), kind=kCustom, calls=%fused_computation.4 | custom fusion | bytes 1048608 | tf_op jit(solution)/shard_map/gather | solution.py:143
  97.1 2.5 %gather_fusion.5 = bf16[8,128,256]{2,1,0:T(8,128)(2,1)} fusion(bf16[8,128,256]{2,1,0:T(8,128)(2,1)} %bitcast.303, s32[1024]{0:T(1024)} %pad_clamp_fusion), kind=kCustom, calls=%fused_computation.5 | custom fusion | bytes 1048608 | tf_op jit(solution)/shard_map/gather | solution.py:144
  99.7 2.1 multiply_reduce_fusion
  101.8 61.4 %reduce-scatter.3.cloned.1.call-done = bf16[128,256]{1,0:T(8,128)(2,1)} async-done(((bf16[1024,256]{1,0:T(8,128)(2,1)}), bf16[128,256]{1,0:T(8,128)(2,1)}) %reduce-scatter.3.cloned.1.call-update) | async-done | bytes 65552 | tf_op jit(solution)/shard_map/reduce_scatter | solution.py:146
  163.2 1.6 multiply_reduce_fusion.2
  166.1 34.9 %reduce-scatter.5.cloned.1.call-done = bf16[128,256]{1,0:T(8,128)(2,1)} async-done(((bf16[1024,256]{1,0:T(8,128)(2,1)}), bf16[128,256]{1,0:T(8,128)(2,1)}) %reduce-scatter.5.cloned.1.call-update) | async-done | bytes 65552 | tf_op jit(solution)/shard_map/reduce_scatter | solution.py:149
  201.0 1.5 multiply_reduce_fusion.1
  204.2 39.2 %psum.7 = f32[]{:T(128)} all-reduce(f32[]{:T(128)S(6)} %add.127), channel_id=1, replica_groups=mesh['head'=4,'seq'=8] {'head','seq'}, use_global_device_ids=true, to_apply=%region_16.17 | all-reduce | flops 1 | bytes 8 | tf_op jit(solution)/shard_map/psum | solution.py:162
  (96 shorter events, 26.5 us)
Async XLA Ops:
  7.2 27.6 %copy-start.16 = (bf16[128,256]{1,0:T(8,128)(2,1)S(1)}, bf16[128,256]{1,0:T(8,128)(2,1)}, u32[]{:S(2)}) copy-start(bf16[128,256]{1,0:T(8,128)(2,1)} %param.17) | copy-start | bytes 196612
  7.2 38.4 %copy-start.17 = (bf16[128,256]{1,0:T(8,128)(2,1)S(1)}, bf16[128,256]{1,0:T(8,128)(2,1)}, u32[]{:S(2)}) copy-start(bf16[128,256]{1,0:T(8,128)(2,1)} %param.13) | copy-start | bytes 196612
  7.2 156.0 %reduce-scatter.3.cloned.1.call-start = ((), (), s32[]{:S(2)}) async-start(), calls=%async_computation.2 | async-start | bytes 589824 | tf_op jit(solution)/shard_map/reduce_scatter | solution.py:146
  23.5 33.2 %copy-start.13 = (bf16[128,2048]{1,0:T(8,128)(2,1)S(1)}, bf16[128,2048]{1,0:T(8,128)(2,1)}, u32[]{:S(2)}) copy-start(bf16[128,2048]{1,0:T(8,128)(2,1)} %param.12) | copy-start | bytes 1572868
  33.7 23.5 %copy-start.14 = (bf16[128,2048]{1,0:T(8,128)(2,1)S(1)}, bf16[128,2048]{1,0:T(8,128)(2,1)}, u32[]{:S(2)}) copy-start(bf16[128,2048]{1,0:T(8,128)(2,1)} %param.15) | copy-start | bytes 1572868
  63.0 1.5 copy-start.9
  63.0 1.5 copy-start.10
  63.0 1.6 copy-start.15
  70.8 3.9 %copy-start.3 = (bf16[128,2,8,128]{0,3,2,1:T(8,128)(2,1)}, bf16[128,2,8,128]{0,3,2,1:T(8,128)(2,1)S(1)}, u32[]{:S(2)}) copy-start(bf16[128,2,8,128]{0,3,2,1:T(8,128)(2,1)S(1)} %get-tuple-element.792) | copy-start | bytes 1572868 | tf_op jit(solution)/shard_map/while
  70.8 4.6 %copy-start.7 = (bf16[1024,256]{0,1:T(8,128)(2,1)}, bf16[1024,256]{0,1:T(8,128)(2,1)S(1)}, u32[]{:S(2)}) copy-start(bf16[1024,256]{0,1:T(8,128)(2,1)S(1)} %get-tuple-element.793) | copy-start | bytes 1572868 | tf_op jit(solution)/shard_map/while
  70.8 2.0 copy-start.12
  74.7 3.8 %copy-start.1 = (bf16[2,8,128,512]{2,3,1,0:T(8,128)(2,1)}, bf16[2,8,128,512]{2,3,1,0:T(8,128)(2,1)S(1)}, u32[]{:S(2)}) copy-start(bf16[2,8,128,512]{2,3,1,0:T(8,128)(2,1)S(1)} %get-tuple-element.676) | copy-start | bytes 6291460 | tf_op jit(solution)/shard_map/while
  75.5 1.0 copy-start.5
  75.5 1.1 copy-start.11
  76.5 1.9 copy-start
  89.1 2.5 copy-start.2
  89.1 2.5 copy-start.6
  91.6 2.9 %copy-start.4 = (bf16[128,2,8,128]{0,3,2,1:T(8,128)(2,1)S(1)}, bf16[128,2,8,128]{0,3,2,1:T(8,128)(2,1)}, u32[]{:S(2)}) copy-start(bf16[128,2,8,128]{0,3,2,1:T(8,128)(2,1)} %copy-done.3) | copy-start | bytes 1572868 | tf_op jit(solution)/shard_map/while
  91.6 2.9 %copy-start.8 = (bf16[1024,256]{0,1:T(8,128)(2,1)S(1)}, bf16[1024,256]{0,1:T(8,128)(2,1)}, u32[]{:S(2)}) copy-start(bf16[1024,256]{0,1:T(8,128)(2,1)} %copy-done.7) | copy-start | bytes 1572868 | tf_op jit(solution)/shard_map/while
  97.1 104.0 %reduce-scatter.5.cloned.1.call-start = ((), (), s32[]{:S(2)}) async-start(), calls=%async_computation.3 | async-start | bytes 589824 | tf_op jit(solution)/shard_map/reduce_scatter | solution.py:149
Sparse Core Ops, SparseCore 0:
  97.2 65.9 reduce-scatter.2
  166.9 34.1 reduce-scatter.4
where the time goes:
time: 251 us; the launch traced here: 250 us
  waiting for transfers between devices  96.4 us (38%)
  blocking collectives  79.2 us (32%)
  local copies, waits for them, and re-layouts  28.2 us (11%)
  matrix products  22.4 us (9%)
  between operations  16.9 us (7%)
  other arithmetic  6.74 us (3%)
    reduce_scatter x1, waiting for transfers between devices, body(): lax.psum_scatter(dk_local.astype(jnp.bfloat16), 'seq', scatter_dimension=...  61.4 us
    psum x1, blocking collectives, body(): squared_norm = lax.psum(local_term, ('head', 'seq'))  39.2 us
    reduce_scatter x1, waiting for transfers between devices, body(): lax.psum_scatter(dv_local.astype(jnp.bfloat16), 'seq', scatter_dimension=...  34.9 us
    all_gather x1, blocking collectives, body(): lax.all_gather(k_tangent, 'seq', axis=0, tiled=True)  11.6 us
    all_gather x1, blocking collectives, body(): lax.all_gather(values, 'seq', axis=0, tiled=True)  9.67 us
    all_gather x1, blocking collectives, body(): lax.all_gather(keys, 'seq', axis=0, tiled=True)  9.5 us
    all_gather x1, blocking collectives, body(): lax.all_gather(v_tangent, 'seq', axis=0, tiled=True)  9.17 us
    unnamed x18, local copies, waits for them, and re-layouts  6.73 us
  transfers between devices with their start and end apart: 2, of which 2 were waited for; matrix products, arithmetic and copies ran while one was open for 2% of the time, Pallas kernels for 0%

commit v1 on v0

--- a/solution.py
+++ b/solution.py
@@ -159,7 +159,8 @@
     local_term = (
         jnp.sum(dq_wide * dq_wide) + jnp.sum(dk_wide * dk_wide) + jnp.sum(dv_wide * dv_wide)
     )
-    squared_norm = lax.psum(local_term, ("head", "seq"))
+    inner = lax.psum(local_term, "seq")
+    squared_norm = lax.psum(inner, "head")
     return (dq_out, dk_out, dv_out, squared_norm)
 
 

time: 251 us -> 237 us (0.944)
  blocking collectives: 79.2 us -> 64.9 us
    psum x1 -> x2, blocking collectives: 39.2 us -> 24.9 us  [the longest x1 12.7 us: body(): inner = lax.psum(local_term, 'seq')]
  transfers between devices with their start and end apart: 2 -> 2, of which waited for: 2 -> 2; matrix products, arithmetic and copies ran while one was open for 2% -> 3% of each run, Pallas kernels for 0% -> 0%
where the time goes in v1:
time: 237 us; the launch traced here: 236 us
  waiting for transfers between devices  96.4 us (41%)
  blocking collectives  64.9 us (27%)
  local copies, waits for them, and re-layouts  28.2 us (12%)
  matrix products  22.4 us (9%)
  between operations  16.9 us (7%)
  other arithmetic  6.74 us (3%)
    reduce_scatter x1, waiting for transfers between devices, body(): lax.psum_scatter(dk_local.astype(jnp.bfloat16), 'seq', scatter_dimension=...  61.4 us
    reduce_scatter x1, waiting for transfers between devices, body(): lax.psum_scatter(dv_local.astype(jnp.bfloat16), 'seq', scatter_dimension=...  34.9 us
    psum x1, blocking collectives, body(): inner = lax.psum(local_term, 'seq')  12.7 us
    psum x1, blocking collectives, body(): squared_norm = lax.psum(inner, 'head')  12.3 us
    all_gather x1, blocking collectives, body(): lax.all_gather(k_tangent, 'seq', axis=0, tiled=True)  11.6 us
    all_gather x1, blocking collectives, body(): lax.all_gather(values, 'seq', axis=0, tiled=True)  9.67 us
    all_gather x1, blocking collectives, body(): lax.all_gather(keys, 'seq', axis=0, tiled=True)  9.5 us
    all_gather x1, blocking collectives, body(): lax.all_gather(v_tangent, 'seq', axis=0, tiled=True)  9.17 us
  transfers between devices with their start and end apart: 2, of which 2 were waited for; matrix products, arithmetic and copies ran while one was open for 3% of the time, Pallas kernels for 0%

profile of v1, /device:TPU:0, one launch (start us, length us, event | category | flops | bytes accessed | tf_op | source)
XLA Modules:
  0.0 235.9 jit_solution(6617886108475450314)
XLA Ops:
  11.0 11.6 %all_gather.13 = bf16[1024,256]{1,0:T(8,128)(2,1)S(1)} all-gather(bf16[128,256]{1,0:T(8,128)(2,1)} %param.16), channel_id=1, replica_groups=mesh['head'=4,'seq'=8] {'seq'}, dimensions={0}, use_global_device_ids=true | all-gather | bytes 589824 | tf_op jit(solution)/shard_map/all_gather | solution.py:100
  23.5 9.7 %all_gather.14 = bf16[1024,256]{1,0:T(8,128)(2,1)S(1)} all-gather(bf16[128,256]{1,0:T(8,128)(2,1)} %param.14), channel_id=1, replica_groups=mesh['head'=4,'seq'=8] {'seq'}, dimensions={0}, use_global_device_ids=true | all-gather | bytes 589824 | tf_op jit(solution)/shard_map/all_gather | solution.py:99
  34.8 9.2 %all_gather.15 = bf16[1024,256]{1,0:T(8,128)(2,1)S(1)} all-gather(bf16[128,256]{1,0:T(8,128)(2,1)S(1)} %copy-done.16), channel_id=1, replica_groups=mesh['head'=4,'seq'=8] {'seq'}, dimensions={0}, use_global_device_ids=true | all-gather | bytes 589824 | tf_op jit(solution)/shard_map/all_gather | solution.py:101
  45.6 9.5 %all_gather.12 = bf16[1024,256]{1,0:T(8,128)(2,1)S(1)} all-gather(bf16[128,256]{1,0:T(8,128)(2,1)S(1)} %copy-done.17), channel_id=1, replica_groups=mesh['head'=4,'seq'=8] {'seq'}, dimensions={0}, use_global_device_ids=true | all-gather | bytes 589824 | tf_op jit(solution)/shard_map/all_gather | solution.py:98
  60.2 7.8 %while.36 = (s32[]{:T(128)}, f32[2,8,128]{2,1,0:T(8,128)S(1)}, f32[2,8,128]{2,1,0:T(8,128)S(1)}, f32[2,8,128]{2,1,0:T(8,128)S(1)}, f32[2,8,128]{2,1,0:T(8,128)S(...) while((s32[]{:T(128)}, f32[2,8,128]{2,1,0:T(8,128)S(1)}, ...), condition=%wide.region_8.9_spmd.clone, body=%wide.region_1.8_spmd.clone.sunk | while | flops 1366372992 | bytes 46478664 | solution.py:120
  64.6 2.1 fusion.114
  70.8 23.7 %while.37 = (s32[]{:T(128)}, f32[128,2,8,128]{0,3,2,1:T(8,128)}, bf16[1024,256]{1,0:T(8,128)(2,1)}, bf16[1024,256]{1,0:T(8,128)(2,1)}, s32[]{:T(128)}, /*index=5...) while((s32[]{:T(128)}, f32[128,2,8,128]{0,3,2,1:T(8,128)}, ...), condition=%wide.region_10.11_spmd.clone, body=%wide.region_9.10_spmd.clone.sunk | while | flops 2704474624 | bytes 123131472 | solution.py:140
  73.0 1.7 multiply_convert_fusion.2
  78.4 1.8 convolution_bitcast_fusion.3
  80.3 1.5 fusion.143
  81.8 1.8 copy.153
  83.6 3.7 %fusion.142 = bf16[2,512,128,1]{1,2,3,0:T(8,128)(2,1)} fusion(bf16[128,2,8,128]{0,3,2,1:T(8,128)(2,1)S(1)} %get-tuple-element.796, f32[2,8,128,512]{2,3,1,0:T(8,128)} %copy-done), kind=kOutput, calls=%fused_computation.47.clone.1 | convolution fusion | flops 269484032 | bytes 4980736 | tf_op jit(solution)/shard_map/while/body/hgts,thgd->shd/dot_general | solution.py:77
  87.3 1.8 copy.152
  89.1 2.0 constant_dynamic-update-slice_fusion.3
  91.6 2.9 %fusion.141 = f32[128,2,8,128]{0,3,2,1:T(8,128)} fusion(f32[128,2,8,128]{0,3,2,1:T(8,128)} %get-tuple-element.762, f32[2,128,8,128]{3,1,2,0:T(8,128)S(1)} %fusion.140, bf16[512,2,128,1]{0,2,3,1:T(8,128)(2,1)S(1)} %bitcast.291, bf16[2,8,128,512]{2,3,1,0:T(8,128)(2,1)S(1)} %copy-done.2), kind=kOutput, calls=%fused_computation.52.clone.1 | convolution fusion | flops 269221888 | bytes 5505024 | tf_op jit(solution)/shard_map/while/body/hgts,shd->thgd/dot_general | solution.py:69
  94.5 2.5 %gather_fusion.4 = bf16[8,128,256]{2,1,0:T(8,128)(2,1)} fusion(bf16[8,128,256]{2,1,0:T(8,128)(2,1)} %bitcast.302, s32[1024]{0:T(1024)} %pad_clamp_fusion), kind=kCustom, calls=%fused_computation.4 | custom fusion | bytes 1048608 | tf_op jit(solution)/shard_map/gather | solution.py:143
  97.1 2.5 %gather_fusion.5 = bf16[8,128,256]{2,1,0:T(8,128)(2,1)} fusion(bf16[8,128,256]{2,1,0:T(8,128)(2,1)} %bitcast.303, s32[1024]{0:T(1024)} %pad_clamp_fusion), kind=kCustom, calls=%fused_computation.5 | custom fusion | bytes 1048608 | tf_op jit(solution)/shard_map/gather | solution.py:144
  99.7 2.1 multiply_reduce_fusion
  101.8 61.4 %reduce-scatter.3.cloned.1.call-done = bf16[128,256]{1,0:T(8,128)(2,1)} async-done(((bf16[1024,256]{1,0:T(8,128)(2,1)}), bf16[128,256]{1,0:T(8,128)(2,1)}) %reduce-scatter.3.cloned.1.call-update) | async-done | bytes 65552 | tf_op jit(solution)/shard_map/reduce_scatter | solution.py:146
  163.2 1.6 multiply_reduce_fusion.2
  166.1 34.9 %reduce-scatter.5.cloned.1.call-done = bf16[128,256]{1,0:T(8,128)(2,1)} async-done(((bf16[1024,256]{1,0:T(8,128)(2,1)}), bf16[128,256]{1,0:T(8,128)(2,1)}) %reduce-scatter.5.cloned.1.call-update) | async-done | bytes 65552 | tf_op jit(solution)/shard_map/reduce_scatter | solution.py:149
  201.0 1.5 multiply_reduce_fusion.1
  203.2 12.7 %psum.14 = f32[]{:T(128)} all-reduce(f32[]{:T(128)S(6)} %add.129), channel_id=1, replica_groups=mesh['head'=4,'seq'=8] {'seq'}, use_global_device_ids=true, to_apply=%region_16.17 | all-reduce | flops 1 | bytes 8 | tf_op jit(solution)/shard_map/psum | solution.py:162
  216.8 12.3 %psum.15 = f32[]{:T(128)} all-reduce(f32[]{:T(128)} %psum.14), channel_id=1, replica_groups=mesh['head'=4,'seq'=8] {'head'}, use_global_device_ids=true, to_apply=%region_17.18 | all-reduce | flops 1 | bytes 8 | tf_op jit(solution)/shard_map/psum | solution.py:163
  (97 shorter events, 27.9 us)
Async XLA Ops:
  7.2 27.6 %copy-start.16 = (bf16[128,256]{1,0:T(8,128)(2,1)S(1)}, bf16[128,256]{1,0:T(8,128)(2,1)}, u32[]{:S(2)}) copy-start(bf16[128,256]{1,0:T(8,128)(2,1)} %param.17) | copy-start | bytes 196612
  7.2 38.4 %copy-start.17 = (bf16[128,256]{1,0:T(8,128)(2,1)S(1)}, bf16[128,256]{1,0:T(8,128)(2,1)}, u32[]{:S(2)}) copy-start(bf16[128,256]{1,0:T(8,128)(2,1)} %param.13) | copy-start | bytes 196612
  7.2 156.0 %reduce-scatter.3.cloned.1.call-start = ((), (), s32[]{:S(2)}) async-start(), calls=%async_computation.2 | async-start | bytes 589824 | tf_op jit(solution)/shard_map/reduce_scatter | solution.py:146
  23.5 33.2 %copy-start.13 = (bf16[128,2048]{1,0:T(8,128)(2,1)S(1)}, bf16[128,2048]{1,0:T(8,128)(2,1)}, u32[]{:S(2)}) copy-start(bf16[128,2048]{1,0:T(8,128)(2,1)} %param.12) | copy-start | bytes 1572868
  33.7 23.5 %copy-start.14 = (bf16[128,2048]{1,0:T(8,128)(2,1)S(1)}, bf16[128,2048]{1,0:T(8,128)(2,1)}, u32[]{:S(2)}) copy-start(bf16[128,2048]{1,0:T(8,128)(2,1)} %param.15) | copy-start | bytes 1572868
  63.0 1.5 copy-start.9
  63.0 1.5 copy-start.10
  63.0 1.6 copy-start.15
  70.8 3.9 %copy-start.3 = (bf16[128,2,8,128]{0,3,2,1:T(8,128)(2,1)}, bf16[128,2,8,128]{0,3,2,1:T(8,128)(2,1)S(1)}, u32[]{:S(2)}) copy-start(bf16[128,2,8,128]{0,3,2,1:T(8,128)(2,1)S(1)} %get-tuple-element.792) | copy-start | bytes 1572868 | tf_op jit(solution)/shard_map/while
  70.8 4.6 %copy-start.7 = (bf16[1024,256]{0,1:T(8,128)(2,1)}, bf16[1024,256]{0,1:T(8,128)(2,1)S(1)}, u32[]{:S(2)}) copy-start(bf16[1024,256]{0,1:T(8,128)(2,1)S(1)} %get-tuple-element.793) | copy-start | bytes 1572868 | tf_op jit(solution)/shard_map/while
  70.8 2.0 copy-start.12
  74.7 3.8 %copy-start.1 = (bf16[2,8,128,512]{2,3,1,0:T(8,128)(2,1)}, bf16[2,8,128,512]{2,3,1,0:T(8,128)(2,1)S(1)}, u32[]{:S(2)}) copy-start(bf16[2,8,128,512]{2,3,1,0:T(8,128)(2,1)S(1)} %get-tuple-element.676) | copy-start | bytes 6291460 | tf_op jit(solution)/shard_map/while
  75.5 1.0 copy-start.5
  75.5 1.1 copy-start.11
  76.5 1.9 copy-start
  89.1 2.5 %copy-start.2 = (bf16[2,8,128,512]{2,3,1,0:T(8,128)(2,1)S(1)}, bf16[2,8,128,512]{2,3,1,0:T(8,128)(2,1)}, u32[]{:S(2)}) copy-start(bf16[2,8,128,512]{2,3,1,0:T(8,128)(2,1)} %copy-done.1) | copy-start | bytes 6291460 | tf_op jit(solution)/shard_map/while
  89.1 2.5 %copy-start.6 = (bf16[512,256]{0,1:T(8,128)(2,1)S(1)}, bf16[512,256]{0,1:T(8,128)(2,1)}, u32[]{:S(2)}) copy-start(bf16[512,256]{0,1:T(8,128)(2,1)} %copy-done.5) | copy-start | bytes 786436 | tf_op jit(solution)/shard_map/while
  91.6 2.9 %copy-start.4 = (bf16[128,2,8,128]{0,3,2,1:T(8,128)(2,1)S(1)}, bf16[128,2,8,128]{0,3,2,1:T(8,128)(2,1)}, u32[]{:S(2)}) copy-start(bf16[128,2,8,128]{0,3,2,1:T(8,128)(2,1)} %copy-done.3) | copy-start | bytes 1572868 | tf_op jit(solution)/shard_map/while
  91.6 2.9 %copy-start.8 = (bf16[1024,256]{0,1:T(8,128)(2,1)S(1)}, bf16[1024,256]{0,1:T(8,128)(2,1)}, u32[]{:S(2)}) copy-start(bf16[1024,256]{0,1:T(8,128)(2,1)} %copy-done.7) | copy-start | bytes 1572868 | tf_op jit(solution)/shard_map/while
  97.1 104.0 %reduce-scatter.5.cloned.1.call-start = ((), (), s32[]{:S(2)}) async-start(), calls=%async_computation.3 | async-start | bytes 589824 | tf_op jit(solution)/shard_map/reduce_scatter | solution.py:149
Sparse Core Ops, SparseCore 0:
  97.2 65.9 reduce-scatter.2
  166.9 34.1 reduce-scatter.4
